TPU v7x, 32 devices: a whole 2x2x4 slice. The times are simulated.
32 devices in a mesh: seq: 8 (over z, x), head: 4 (over y, core).
Axes of the slice: x: 2, y: 2, z: 4, core: 2. Of those that a mesh axis runs over, the one named last changes fastest.
Arguments:
- q_latent: bfloat16 [2048, 1536], P('seq', 'head'), may hold values from -6 to 6
- kv_latent: bfloat16 [2048, 512], P('seq', 'head'), may hold values from -6 to 6
- k_rope: bfloat16 [2048, 64], P('seq'), may hold values from -6 to 6
- segment_ids: int32 [2048], P('seq'), may hold values from 0 to 7, as said below
- w_q_nope: bfloat16 [1536, 16384], P('seq', 'head'), may hold values from -6 to 6
- w_q_rope: bfloat16 [1536, 8192], P('seq', 'head'), may hold values from -6 to 6
- w_kv_nope: bfloat16 [512, 16384], P('seq', 'head'), may hold values from -6 to 6
- threshold: float32 [1], replicated, may hold values from 3.5 to 5.5
Outputs:
- new_q_nope: bfloat16 [1536, 16384], P('seq', 'head')
- new_q_rope: bfloat16 [1536, 8192], P('seq', 'head')
- new_kv_nope: bfloat16 [512, 16384], P('seq', 'head')
- head_max: float32 [128], P('head')
- row_max: float32 [2048, 128], P('seq', 'head')
Inputs may be any that keep to these rules, and one draw needn't show every extreme that they name: segment_ids never fall along the tokens and each document has 1 to 768 tokens.
All inputs are finite; a program needn't handle non-finite values.
Results may differ from a plain program's by a relative error of at most 0.0034.
Values may be sent and summed in bfloat16 or wider, within the bound.
A program may use at most 128 MiB of HBM per device.

v0:
```python
import math
import jax
import jax.numpy as jnp
from jax import lax
from jax.sharding import PartitionSpec as P

D_NOPE = 128
D_ROPE = 64
QLORA = 1536
KVLORA = 512
REACH = 3


def as_sent(value):
    return jax.tree.map(lambda a: a.astype(jnp.bfloat16) if a.dtype == jnp.float32 else a, value)


def from_partner(value, axis, stride):
    mask = 2**stride
    pairs = [(source, source ^ mask) for source in range(lax.axis_size(axis))]
    return lax.ppermute(value, axis, pairs)


def shifted(block, axis, distance):
    devices = range(lax.axis_size(axis))
    route = [(i - distance, i) for i in devices if i - distance in devices]
    return lax.ppermute(block, axis, route)


def score_max(query_nope, query_rope, key_nope, key_rope, allowed):
    nope = jnp.einsum("qhd,khd->hqk", query_nope, key_nope, preferred_element_type=jnp.float32)
    rope = jnp.einsum("qhd,kd->hqk", query_rope, key_rope, preferred_element_type=jnp.float32)
    scores = (nope + rope) * (1.0 / math.sqrt(D_NOPE + D_ROPE))
    return jnp.max(jnp.where(allowed[None], scores, jnp.float32(-1e30)), axis=2)


def masked_max(compute, operands):
    return compute(*operands)


def spread_columns(weight, width, quarter, copies):
    pieces = weight.reshape(weight.shape[0], 4, quarter * width).transpose(1, 0, 2)
    return jnp.tile(pieces, (copies, 1, 1))


def body(q_latent, kv_latent, k_rope, segment_ids, w_q_nope, w_q_rope, w_kv_nope, threshold):
    q_whole, kv_whole = (
        lax.all_gather(q_latent, "head", axis=1, tiled=True),
        lax.all_gather(kv_latent, "head", axis=1, tiled=True),
    )
    rows = q_whole.shape[0]
    heads = w_q_nope.shape[1] // D_NOPE
    q_scale = 1.0 / math.sqrt(QLORA)
    k_scale = 1.0 / math.sqrt(KVLORA)
    place = lax.axis_index("seq")
    quarter = heads // 4
    copies = lax.axis_size("seq") // 4
    slot = place % 4
    sent = (
        spread_columns(w_q_nope, D_NOPE, quarter, copies),
        spread_columns(w_q_rope, D_ROPE, quarter, copies),
        spread_columns(w_kv_nope, D_NOPE, quarter, copies),
    )
    got_nope, got_rope, got_kv = (
        lax.all_to_all(sent[0], "seq", split_axis=0, concat_axis=1, tiled=True),
        lax.all_to_all(sent[1], "seq", split_axis=0, concat_axis=1, tiled=True),
        lax.all_to_all(sent[2], "seq", split_axis=0, concat_axis=1, tiled=True),
    )
    sub_nope = got_nope.reshape(QLORA, quarter * D_NOPE)
    sub_rope = got_rope.reshape(QLORA, quarter * D_ROPE)
    sub_kv = got_kv.reshape(KVLORA, quarter * D_NOPE)
    group = (q_whole, kv_whole, k_rope)
    for level in range(2):
        partner = jax.tree.map(
            lambda part, own: part.astype(own.dtype),
            from_partner(as_sent(group), "seq", level),
            group,
        )
        upper = place // (1 << level) % 2 == 1
        group = tuple(
            (
                jnp.where(
                    upper, jnp.concatenate([other, mine], 0), jnp.concatenate([mine, other], 0)
                )
                for mine, other in zip(group, partner)
            )
        )
    group_q, group_kv, group_rope = group
    early_kv, early_rope = shifted(
        (group_kv[(4 - REACH) * rows :], group_rope[(4 - REACH) * rows :]), "seq", 4
    )
    keys_kv = jnp.concatenate([early_kv, group_kv], 0)
    keys_rope = jnp.concatenate([early_rope, group_rope], 0)
    key_nope = (
        (jnp.dot(keys_kv, sub_kv, preferred_element_type=jnp.float32) * k_scale)
        .astype(jnp.bfloat16)
        .reshape(keys_kv.shape[0], quarter, D_NOPE)
    )
    query_nope = (
        (jnp.dot(group_q, sub_nope, preferred_element_type=jnp.float32) * q_scale)
        .astype(jnp.bfloat16)
        .reshape(4 * rows, quarter, D_NOPE)
    )
    query_rope = (
        (jnp.dot(group_q, sub_rope, preferred_element_type=jnp.float32) * q_scale)
        .astype(jnp.bfloat16)
        .reshape(4 * rows, quarter, D_ROPE)
    )
    all_segs = lax.all_gather(segment_ids, "seq", axis=0, tiled=True)
    padded_segs = jnp.concatenate([jnp.full((REACH * rows,), -1, jnp.int32), all_segs], 0)
    first = place // 4 * 4
    window = (REACH + 1) * rows
    block_rows = []
    for local in range(4):
        block = first + local
        query_seg = lax.dynamic_slice_in_dim(all_segs, block * rows, rows, 0)
        key_seg = lax.dynamic_slice_in_dim(padded_segs, block * rows, window, 0)
        query_pos = block * rows + jnp.arange(rows, dtype=jnp.int32)
        key_pos = (block - REACH) * rows + jnp.arange(window, dtype=jnp.int32)
        allowed = (
            (query_seg[:, None] == key_seg[None, :])
            & (key_pos[None, :] <= query_pos[:, None])
            & (key_pos[None, :] >= 0)
        )
        operands = (
            query_nope[local * rows : (local + 1) * rows],
            query_rope[local * rows : (local + 1) * rows],
            key_nope[local * rows : local * rows + window],
            keys_rope[local * rows : local * rows + window],
            allowed,
        )
        block_rows.append(masked_max(score_max, operands))
    stacked = jnp.stack(block_rows, 0)[None]
    for level in range(2):
        partner = from_partner(stacked, "seq", level)
        upper = place // (1 << level) % 2 == 1
        stacked = jnp.where(
            upper, jnp.concatenate([partner, stacked], 0), jnp.concatenate([stacked, partner], 0)
        )
    own = lax.dynamic_index_in_dim(stacked, slot, 1, False)
    row_max = own.reshape(heads, rows).T
    local_heads = jnp.max(row_max, axis=0)
    head_max = lax.pmax(local_heads, "seq")
    clip = threshold[0] / jnp.maximum(head_max, threshold[0])
    root = jnp.sqrt(clip)
    new_q_nope = (w_q_nope.astype(jnp.float32) * jnp.repeat(root, D_NOPE)[None, :]).astype(
        jnp.bfloat16
    )
    new_q_rope = (w_q_rope.astype(jnp.float32) * jnp.repeat(clip, D_ROPE)[None, :]).astype(
        jnp.bfloat16
    )
    new_kv_nope = (w_kv_nope.astype(jnp.float32) * jnp.repeat(root, D_NOPE)[None, :]).astype(
        jnp.bfloat16
    )
    return (new_q_nope, new_q_rope, new_kv_nope, head_max, row_max)


def solution(mesh):
    in_specs = (
        P("seq", "head"),
        P("seq", "head"),
        P("seq", None),
        P("seq"),
        P("seq", "head"),
        P("seq", "head"),
        P("seq", "head"),
        P(),
    )
    out_specs = (P("seq", "head"), P("seq", "head"), P("seq", "head"), P("head"), P("seq", "head"))
    return jax.shard_map(body, mesh=mesh, in_specs=in_specs, out_specs=out_specs, check_vma=False)
```

profile of v0, /device:TPU:0, one launch (start us, length us, event | category | flops | bytes accessed | tf_op | source)
XLA Modules:
  0.0 299.3 jit_solution(7385676597361516628)
XLA Ops:
  0.6 1.5 reshape.406
  2.3 1.1 tile.14
  3.4 7.3 %all-to-all-start.1 = ((bf16[8,64,1024]{2,1,0:T(8,128)(2,1)}), bf16[8,64,1024]{2,1,0:T(8,128)(2,1)S(1)}, u32[]{:S(2)}, u32[]{:S(2)}) async-start(bf16[8,64,1024]{2,1,0:T(8,128)(2,1)} %bitcast.8), calls=%async_computation.1 | async-start | bytes 2097152 | tf_op jit(solution)/shard_map/all_to_all | solution.py:67
  11.4 25.0 %all-to-all-done.1 = bf16[8,64,1024]{2,1,0:T(8,128)(2,1)S(1)} async-done(((bf16[8,64,1024]{2,1,0:T(8,128)(2,1)}), bf16[8,64,1024]{2,1,0:T(8,128)(2,1)S(1)}, u32[]{:S(2)}, u32[]{:S(2)}) %all-to-all-start.1) | async-done | bytes 1048608 | tf_op jit(solution)/shard_map/all_to_all | solution.py:67
  36.5 1.4 tile.31
  37.9 4.3 %all-to-all-start.2 = ((bf16[8,192,512]{2,1,0:T(8,128)(2,1)}), bf16[8,192,512]{2,1,0:T(8,128)(2,1)}, u32[]{:S(2)}, u32[]{:S(2)}) async-start(bf16[8,192,512]{2,1,0:T(8,128)(2,1)} %bitcast.13), calls=%async_computation.2 | async-start | bytes 3145728 | tf_op jit(solution)/shard_map/all_to_all | solution.py:66
  42.3 1.2 reshape.404
  43.9 34.9 %all-to-all-done.2 = bf16[8,192,512]{2,1,0:T(8,128)(2,1)} async-done(((bf16[8,192,512]{2,1,0:T(8,128)(2,1)}), bf16[8,192,512]{2,1,0:T(8,128)(2,1)}, u32[]{:S(2)}, u32[]{:S(2)}) %all-to-all-start.2) | async-done | bytes 1572896 | tf_op jit(solution)/shard_map/all_to_all | solution.py:66
  78.8 2.1 tile.12
  81.0 4.6 %all-to-all-start = ((bf16[8,192,1024]{2,1,0:T(8,128)(2,1)}), bf16[8,192,1024]{2,1,0:T(8,128)(2,1)}, u32[]{:S(2)}, u32[]{:S(2)}) async-start(bf16[8,192,1024]{2,1,0:T(8,128)(2,1)} %bitcast.4), calls=%async_computation | async-start | bytes 6291456 | tf_op jit(solution)/shard_map/all_to_all | solution.py:65
  85.6 1.9 collective-permute-start.5
  87.5 5.8 %all_gather.11 = bf16[256,512]{1,0:T(8,128)(2,1)S(1)} all-gather(bf16[256,128]{1,0:T(8,128)(2,1)S(1)} %copy-done.15), channel_id=1, replica_groups=mesh['seq'=8,'head'=4] {'head'}, dimensions={1}, use_global_device_ids=true | all-gather | bytes 327680 | tf_op jit(solution)/shard_map/all_gather | solution.py:49
  93.5 8.6 %all_gather.10 = bf16[256,1536]{1,0:T(8,128)(2,1)S(1)} all-gather(bf16[256,384]{1,0:T(8,128)(2,1)S(1)} %copy-done.14), channel_id=1, replica_groups=mesh['seq'=8,'head'=4] {'head'}, dimensions={1}, use_global_device_ids=true | all-gather | bytes 983040 | tf_op jit(solution)/shard_map/all_gather | solution.py:48
  102.1 1.8 collective-permute-start
  104.0 50.2 %all-gather = s32[8,1,256]{2,1,0:T(1,128)S(1)} all-gather(s32[1,1,256]{2,1,0:T(1,128)S(1)} %bitcast.118), channel_id=1, replica_groups=mesh['seq'=8,'head'=4] {'seq'}, dimensions={0}, use_global_device_ids=true | all-gather | bytes 9216 | tf_op jit(solution)/shard_map/all_gather | solution.py:109
  154.6 11.1 %collective-permute-start.3 = (bf16[512,512]{1,0:T(8,128)(2,1)S(1)}, bf16[512,512]{1,0:T(8,128)(2,1)S(1)}, u32[]{:S(2)}, u32[]{:S(2)}) collective-permute-start(bf16[512,512]{1,0:T(8,128)(2,1)S(1)} %maximum_select_fusion.5), channel_id=1, source_target_pairs={{0,8},{4,12},{8,0},{12,4},{16,24},{20,28},{24,16},{28,20},{1,9},{5... | collective-permute-start | bytes 1572872 | tf_op jit(solution)/shard_map/ppermute | solution.py:21
  166.0 1.2 and_and_fusion.1
  167.3 6.2 %collective-permute-done.3 = bf16[512,512]{1,0:T(8,128)(2,1)S(1)} collective-permute-done((bf16[512,512]{1,0:T(8,128)(2,1)S(1)}, bf16[512,512]{1,0:T(8,128)(2,1)S(1)}, u32[]{:S(2)}, u32[]{:S(2)}) %collective-permute-start.3) | collective-permute-done | bytes 524320 | tf_op jit(solution)/shard_map/ppermute | solution.py:21
  174.1 4.7 %collective-permute-start.4 = (bf16[768,512]{1,0:T(8,128)(2,1)S(1)}, bf16[768,512]{1,0:T(8,128)(2,1)S(1)}, u32[]{:S(2)}, u32[]{:S(2)}) collective-permute-start(bf16[768,512]{1,0:T(8,128)(2,1)S(1)} %slice.117), channel_id=1, source_target_pairs={{0,16},{4,20},{8,24},{12,28},{1,17},{5,21},{9,25},{13,29},{2,18},{... | collective-permute-start | bytes 2359304 | tf_op jit(solution)/shard_map/ppermute | solution.py:27
  178.8 0.6 maximum_select_fusion.1
  179.4 0.6 collective-permute-start.1
  180.1 1.5 collective-permute-start.6
  182.0 44.8 %collective-permute-done.6 = bf16[512,64]{0,1:T(8,128)(2,1)S(1)} collective-permute-done((bf16[512,64]{0,1:T(8,128)(2,1)S(1)}, bf16[512,64]{0,1:T(8,128)(2,1)S(1)}, u32[]{:S(2)}, u32[]{:S(2)}) %collective-permute-start.6) | collective-permute-done | bytes 65568 | tf_op jit(solution)/shard_map/ppermute | solution.py:21
  226.8 0.6 slice.119
  227.4 2.1 collective-permute-start.7
  229.6 2.2 multiply_convert_fusion
  231.8 3.0 fusion.37
  234.7 3.9 %multiply_convert_fusion.3 = bf16[1024,512]{0,1:T(8,128)(2,1)S(1)} fusion(bf16[1536,512]{1,0:T(8,128)(2,1)} %bitcast.14, bf16[512,1536]{1,0:T(8,128)(2,1)S(1)} %maximum_select_fusion.1, bf16[512,1536]{1,0:T(8,128)(2,1)S(1)} %collective-permute-done.1, pred[]{:T(512)S(6)} %eq.82), kind=kOutput, calls=%fused_computation.20 | convolution fusion | flops 1625817088 | bytes 5767169 | tf_op jit(solution)/shard_map/dot_general | solution.py:105
  238.6 0.9 fusion.39
  239.5 7.3 %multiply_convert_fusion.1 = bf16[1024,1024]{0,1:T(8,128)(2,1)S(1)} fusion(bf16[1536,1024]{1,0:T(8,128)(2,1)} %bitcast.5, bf16[512,1536]{1,0:T(8,128)(2,1)} %copy-done.8, bf16[512,1536]{1,0:T(8,128)(2,1)} %copy-done.19, pred[]{:T(512)S(6)} %eq.82), kind=kOutput, calls=%fused_computation.17 | convolution fusion | flops 3237478400 | bytes 8388609 | tf_op jit(solution)/shard_map/dot_general | solution.py:100
  246.9 1.4 copy-done.2
  248.4 1.3 fusion.44
  250.0 1.3 fusion.41
  251.5 1.3 fusion.43
  252.9 2.1 fusion.2
  255.0 1.5 fusion.42
  256.5 3.0 %fusion.11 = f32[8,256]{1,0:T(8,128)S(1)} fusion(f32[8,256,1024]{2,1,0:T(8,128)S(1)} %fusion.41, pred[256,1024]{1,0:T(8,128)(4,1)S(1)} %and_and_fusion.3, bf16[256,8,64]{0,2,1:T(8,128)(2,1)S(1)} %bitcast.109, bf16[1024,64]{0,1:T(8,128)(2,1)S(1)} %maximum_select_fusion.6, bf16[768,64]{0,1:T(8,128)(2,1)} %collective-permute-done.7), kind=kOutput, calls=%fused_computation.15 | convolution fusion | flops 277084160 | bytes 9150464 | tf_op jit(solution)/shard_map/qhd,kd->hqk/dot_general | solution.py:32
  259.6 2.9 fusion.5
  262.5 3.1 %fusion.8 = f32[8,256]{1,0:T(8,128)S(1)} fusion(f32[8,256,1024]{2,1,0:T(8,128)S(1)} %fusion.42, pred[256,1024]{1,0:T(8,128)(4,1)S(1)} %get-tuple-element.30, bf16[256,8,64]{0,2,1:T(8,128)(2,1)S(1)} %bitcast.107, bf16[1024,64]{0,1:T(8,128)(2,1)S(1)} %maximum_select_fusion.6, bf16[768,64]{0,1:T(8,128)(2,1)} %collective-permute-done.7), kind=kOutput, calls=%fused_computation.11 | convolution fusion | flops 277084160 | bytes 9150464 | tf_op jit(solution)/shard_map/qhd,kd->hqk/dot_general | solution.py:32
  265.7 3.4 %collective-permute-start.8 = (f32[1,4,8,256]{3,2,0,1:T(8,128)S(1)}, f32[1,4,8,256]{3,2,0,1:T(8,128)S(1)}, u32[]{:S(2)}, u32[]{:S(2)}) collective-permute-start(f32[1,4,8,256]{3,2,0,1:T(8,128)S(1)} %maximum_bitcast_fusion), channel_id=1, source_target_pairs={{0,4},{4,0},{8,12},{12,8},{16,20},{20,16},{24,28},{28,24},{1,5},{5... | collective-permute-start | bytes 98312 | tf_op jit(solution)/shard_map/ppermute | solution.py:21
  269.1 1.9 collective-permute-done.8
  271.0 2.5 collective-permute-start.9
  274.2 1.6 collective-permute-done.9
  275.8 0.6 fusion.35
  276.5 19.1 %pmax.7 = f32[32]{0:T(128)S(1)} all-reduce(f32[32]{0:T(128)S(1)} %reduce_max.52), channel_id=1, replica_groups=mesh['seq'=8,'head'=4] {'seq'}, use_global_device_ids=true, to_apply=%region_5.6 | all-reduce | flops 32 | bytes 256 | tf_op jit(solution)/shard_map/pmax | solution.py:143
  295.7 0.9 multiply_convert_fusion.5
  296.6 1.5 multiply_convert_fusion.2
  298.2 1.0 multiply_convert_fusion.4
  (80 shorter events, 4.4 us)
Async XLA Ops:
  0.6 10.1 %copy-start.5 = (bf16[192,2048]{1,0:T(8,128)(2,1)S(1)}, bf16[192,2048]{1,0:T(8,128)(2,1)}, u32[]{:S(2)}) copy-start(bf16[192,2048]{1,0:T(8,128)(2,1)} %param.13) | copy-start | bytes 2359300
  3.4 33.0 %all-to-all-start.1 = ((bf16[8,64,1024]{2,1,0:T(8,128)(2,1)}), bf16[8,64,1024]{2,1,0:T(8,128)(2,1)S(1)}, u32[]{:S(2)}, u32[]{:S(2)}) async-start(bf16[8,64,1024]{2,1,0:T(8,128)(2,1)} %bitcast.8), calls=%async_computation.1 | async-start | bytes 2097152 | tf_op jit(solution)/shard_map/all_to_all | solution.py:67
  11.4 30.8 %copy-start.3 = (bf16[192,4096]{1,0:T(8,128)(2,1)S(1)}, bf16[192,4096]{1,0:T(8,128)(2,1)}, u32[]{:S(2)}) copy-start(bf16[192,4096]{1,0:T(8,128)(2,1)} %param.12) | copy-start | bytes 4718596
  36.5 1.5 copy-start.9
  37.9 40.9 %all-to-all-start.2 = ((bf16[8,192,512]{2,1,0:T(8,128)(2,1)}), bf16[8,192,512]{2,1,0:T(8,128)(2,1)}, u32[]{:S(2)}, u32[]{:S(2)}) async-start(bf16[8,192,512]{2,1,0:T(8,128)(2,1)} %bitcast.13), calls=%async_computation.2 | async-start | bytes 3145728 | tf_op jit(solution)/shard_map/all_to_all | solution.py:66
  80.9 4.6 %copy-start.16 = (bf16[256,64]{0,1:T(8,128)(2,1)S(1)}, bf16[256,64]{0,1:T(8,128)(2,1)}, u32[]{:S(2)}) copy-start(bf16[256,64]{0,1:T(8,128)(2,1)} %param.10) | copy-start | bytes 98308
  80.9 6.5 %copy-start.15 = (bf16[256,128]{1,0:T(8,128)(2,1)S(1)}, bf16[256,128]{1,0:T(8,128)(2,1)}, u32[]{:S(2)}) copy-start(bf16[256,128]{1,0:T(8,128)(2,1)} %param.9) | copy-start | bytes 196612
  80.9 12.5 %copy-start.14 = (bf16[256,384]{1,0:T(8,128)(2,1)S(1)}, bf16[256,384]{1,0:T(8,128)(2,1)}, u32[]{:S(2)}) copy-start(bf16[256,384]{1,0:T(8,128)(2,1)} %param.8) | copy-start | bytes 589828
  81.0 23.1 %copy-start.17 = (s32[256]{0:T(256)S(1)}, s32[256]{0:T(256)}, u32[]{:S(2)}) copy-start(s32[256]{0:T(256)} %param.11) | copy-start | bytes 3076
  81.0 158.5 %all-to-all-start = ((bf16[8,192,1024]{2,1,0:T(8,128)(2,1)}), bf16[8,192,1024]{2,1,0:T(8,128)(2,1)}, u32[]{:S(2)}, u32[]{:S(2)}) async-start(bf16[8,192,1024]{2,1,0:T(8,128)(2,1)} %bitcast.4), calls=%async_computation | async-start | bytes 6291456 | tf_op jit(solution)/shard_map/all_to_all | solution.py:65
  85.6 94.5 %collective-permute-start.5 = (bf16[256,64]{0,1:T(8,128)(2,1)S(1)}, bf16[256,64]{0,1:T(8,128)(2,1)S(1)}, u32[]{:S(2)}, u32[]{:S(2)}) collective-permute-start(bf16[256,64]{0,1:T(8,128)(2,1)S(1)} %copy-done.16), channel_id=1, source_target_pairs={{0,4},{4,0},{8,12},{12,8},{16,20},{20,16},{24,28},{28,24},{1,5},{5... | collective-permute-start | bytes 98312 | tf_op jit(solution)/shard_map/ppermute | solution.py:21
  93.3 61.1 %collective-permute-start.2 = (bf16[256,512]{1,0:T(8,128)(2,1)S(1)}, bf16[256,512]{1,0:T(8,128)(2,1)S(1)}, u32[]{:S(2)}, u32[]{:S(2)}) collective-permute-start(bf16[256,512]{1,0:T(8,128)(2,1)S(1)} %all_gather.11), channel_id=1, source_target_pairs={{0,4},{4,0},{8,12},{12,8},{16,20},{20,16},{24,28},{28,24},{1,5},{5... | collective-permute-start | bytes 786440 | tf_op jit(solution)/shard_map/ppermute | solution.py:21
  102.1 76.7 %collective-permute-start = (bf16[256,1536]{1,0:T(8,128)(2,1)S(1)}, bf16[256,1536]{1,0:T(8,128)(2,1)S(1)}, u32[]{:S(2)}, u32[]{:S(2)}) collective-permute-start(bf16[256,1536]{1,0:T(8,128)(2,1)S(1)} %all_gather.10), channel_id=1, source_target_pairs={{0,4},{4,0},{8,12},{12,8},{16,20},{20,16},{24,28},{28,24},{1,5},{5... | collective-permute-start | bytes 2359304 | tf_op jit(solution)/shard_map/ppermute | solution.py:21
  154.6 18.9 %collective-permute-start.3 = (bf16[512,512]{1,0:T(8,128)(2,1)S(1)}, bf16[512,512]{1,0:T(8,128)(2,1)S(1)}, u32[]{:S(2)}, u32[]{:S(2)}) collective-permute-start(bf16[512,512]{1,0:T(8,128)(2,1)S(1)} %maximum_select_fusion.5), channel_id=1, source_target_pairs={{0,8},{4,12},{8,0},{12,4},{16,24},{20,28},{24,16},{28,20},{1,9},{5... | collective-permute-start | bytes 1572872 | tf_op jit(solution)/shard_map/ppermute | solution.py:21
  174.0 55.6 %copy-start.10 = (bf16[8,64,1024]{2,1,0:T(8,128)(2,1)S(1)}, bf16[8,64,1024]{2,1,0:T(8,128)(2,1)}, u32[]{:S(2)}) copy-start(bf16[8,64,1024]{2,1,0:T(8,128)(2,1)} %copy-done.9) | copy-start | bytes 3145732
  174.1 55.5 %collective-permute-start.4 = (bf16[768,512]{1,0:T(8,128)(2,1)S(1)}, bf16[768,512]{1,0:T(8,128)(2,1)S(1)}, u32[]{:S(2)}, u32[]{:S(2)}) collective-permute-start(bf16[768,512]{1,0:T(8,128)(2,1)S(1)} %slice.117), channel_id=1, source_target_pairs={{0,16},{4,20},{8,24},{12,28},{1,17},{5,21},{9,25},{13,29},{2,18},{... | collective-permute-start | bytes 2359304 | tf_op jit(solution)/shard_map/ppermute | solution.py:27
  179.4 55.3 %copy-start.8 = (bf16[512,1536]{1,0:T(8,128)(2,1)}, bf16[512,1536]{1,0:T(8,128)(2,1)S(1)}, u32[]{:S(2)}) copy-start(bf16[512,1536]{1,0:T(8,128)(2,1)S(1)} %maximum_select_fusion.1) | copy-start | bytes 4718596
  179.4 55.3 %collective-permute-start.1 = (bf16[512,1536]{1,0:T(8,128)(2,1)S(1)}, bf16[512,1536]{1,0:T(8,128)(2,1)S(1)}, u32[]{:S(2)}, u32[]{:S(2)}) collective-permute-start(bf16[512,1536]{1,0:T(8,128)(2,1)S(1)} %maximum_select_fusion.1), channel_id=1, source_target_pairs={{0,8},{4,12},{8,0},{12,4},{16,24},{20,28},{24,16},{28,20},{1,9},{5... | collective-permute-start | bytes 4718600 | tf_op jit(solution)/shard_map/ppermute | solution.py:21
  180.1 46.6 %collective-permute-start.6 = (bf16[512,64]{0,1:T(8,128)(2,1)S(1)}, bf16[512,64]{0,1:T(8,128)(2,1)S(1)}, u32[]{:S(2)}, u32[]{:S(2)}) collective-permute-start(bf16[512,64]{0,1:T(8,128)(2,1)S(1)} %maximum_select_fusion.7), channel_id=1, source_target_pairs={{0,8},{4,12},{8,0},{12,4},{16,24},{20,28},{24,16},{28,20},{1,9},{5... | collective-permute-start | bytes 196616 | tf_op jit(solution)/shard_map/ppermute | solution.py:21
  227.4 29.1 %collective-permute-start.7 = (bf16[768,64]{0,1:T(8,128)(2,1)}, bf16[768,64]{0,1:T(8,128)(2,1)}, u32[]{:S(2)}, u32[]{:S(2)}) collective-permute-start(bf16[768,64]{0,1:T(8,128)(2,1)} %slice.119), channel_id=1, source_target_pairs={{0,16},{4,20},{8,24},{12,28},{1,17},{5,21},{9,25},{13,29},{2,18},{... | collective-permute-start | bytes 294920 | tf_op jit(solution)/shard_map/ppermute | solution.py:27
  234.7 3.9 %copy-start.19 = (bf16[512,1536]{1,0:T(8,128)(2,1)}, bf16[512,1536]{1,0:T(8,128)(2,1)S(1)}, u32[]{:S(2)}) copy-start(bf16[512,1536]{1,0:T(8,128)(2,1)S(1)} %collective-permute-done.1) | copy-start | bytes 4718596
  246.8 1.6 copy-start.2
  248.4 1.6 copy-start.1
  250.0 1.6 copy-start
  251.5 1.3 copy-start.13
  256.5 3.1 %copy-start.11 = (pred[256,1024]{1,0:T(8,128)(4,1)S(1)}, pred[256,1024]{1,0:T(8,128)(4,1)}, u32[]{:S(2)}) copy-start(pred[256,1024]{1,0:T(8,128)(4,1)} %get-tuple-element.29) | copy-start | bytes 786436
  259.6 2.9 copy-start.12
  262.5 33.2 %copy-start.7 = (bf16[64,4096]{1,0:T(8,128)(2,1)S(1)}, bf16[64,4096]{1,0:T(8,128)(2,1)}, u32[]{:S(2)}) copy-start(bf16[64,4096]{1,0:T(8,128)(2,1)} %param.14) | copy-start | bytes 1572868
  262.5 34.1 %copy-start.4 = (bf16[192,4096]{1,0:T(8,128)(2,1)S(1)}, bf16[192,4096]{1,0:T(8,128)(2,1)}, u32[]{:S(2)}) copy-start(bf16[192,4096]{1,0:T(8,128)(2,1)} %param.12) | copy-start | bytes 4718596
  265.7 32.6 %copy-start.6 = (bf16[192,2048]{1,0:T(8,128)(2,1)S(1)}, bf16[192,2048]{1,0:T(8,128)(2,1)}, u32[]{:S(2)}) copy-start(bf16[192,2048]{1,0:T(8,128)(2,1)} %param.13) | copy-start | bytes 2359300
  265.7 5.3 %collective-permute-start.8 = (f32[1,4,8,256]{3,2,0,1:T(8,128)S(1)}, f32[1,4,8,256]{3,2,0,1:T(8,128)S(1)}, u32[]{:S(2)}, u32[]{:S(2)}) collective-permute-start(f32[1,4,8,256]{3,2,0,1:T(8,128)S(1)} %maximum_bitcast_fusion), channel_id=1, source_target_pairs={{0,4},{4,0},{8,12},{12,8},{16,20},{20,16},{24,28},{28,24},{1,5},{5... | collective-permute-start | bytes 98312 | tf_op jit(solution)/shard_map/ppermute | solution.py:21
  271.0 4.8 %collective-permute-start.9 = (f32[2,4,8,256]{3,2,0,1:T(8,128)S(1)}, f32[2,4,8,256]{3,2,0,1:T(8,128)S(1)}, u32[]{:S(2)}, u32[]{:S(2)}) collective-permute-start(f32[2,4,8,256]{3,2,0,1:T(8,128)S(1)} %maximum_select_fusion.8), channel_id=1, source_target_pairs={{0,8},{4,12},{8,0},{12,4},{16,24},{20,28},{24,16},{28,20},{1,9},{5... | collective-permute-start | bytes 196616 | tf_op jit(solution)/shard_map/ppermute | solution.py:21
  295.6 3.6 %copy-start.18 = (f32[32]{0:T(128)}, f32[32]{0:T(128)S(1)}, u32[]{:S(2)}) copy-start(f32[32]{0:T(128)S(1)} %pmax.7) | copy-start | bytes 388
where the time goes:
time: 300 us; the launch traced here: 299 us
  waiting for transfers between devices  114 us (38%)
  blocking collectives  83.7 us (28%)
  starting transfers between devices  46.2 us (15%)
  matrix products  29.9 us (10%)
  local copies, waits for them, and re-layouts  16 us (5%)
  other arithmetic  7.27 us (2%)
    ppermute x8, waiting for transfers between devices, from_partner(): return lax.ppermute(value, axis, pairs)  54.5 us
    all_gather x1, blocking collectives, body(): all_segs = lax.all_gather(segment_ids, 'seq', axis=0, tiled=True)  50.2 us
    all_to_all x1, waiting for transfers between devices, body(): lax.all_to_all(sent[1], 'seq', split_axis=0, concat_axis=1, tiled=True)  34.9 us
    all_to_all x1, waiting for transfers between devices, body(): lax.all_to_all(sent[2], 'seq', split_axis=0, concat_axis=1, tiled=True)  25 us
    ppermute x8, starting transfers between devices, from_partner(): return lax.ppermute(value, axis, pairs)  23.1 us
    pmax x1, blocking collectives, body(): head_max = lax.pmax(local_heads, 'seq')  19.1 us
    dot_general x4, matrix products, score_max(): jnp.einsum('qhd,kd->hqk', query_rope, key_rope, preferred_element_type=jn...  11.2 us
    all_gather x1, blocking collectives, body(): lax.all_gather(q_latent, 'head', axis=1, tiled=True)  8.59 us
  transfers between devices with their start and end apart: 13, of which 6 were waited for; matrix products, arithmetic and copies ran while one was open for 10% of the time, Pallas kernels for 0%

commit v1 on v0

--- a/solution.py
+++ b/solution.py
@@ -1,3 +1,4 @@
+import functools
 import math
 import jax
 import jax.numpy as jnp
@@ -9,6 +10,27 @@
 QLORA = 1536
 KVLORA = 512
 REACH = 3
+
+
+def unit_put(content, device_axis):
+    workers = lax.axis_size(device_axis)
+    z2 = range(workers)
+    view_out = map(lambda idx: (idx, (idx + 1) % workers), z2)
+    ledger = list(view_out)
+
+    def extend_types_up(passed):
+        if len(passed) == workers:
+            return passed
+        val2 = lax.ppermute(passed[0], device_axis, ledger)
+        return extend_types_up([val2, *passed])
+
+    heard = extend_types_up([content])
+    v1 = jnp.concatenate(heard, axis=0)
+    n_now = lax.axis_index(device_axis)
+    return jnp.roll(v1, shift=(n_now + 1) * content.shape[0], axis=0)
+
+
+find_matrix_now = functools.partial(unit_put, device_axis="seq")
 
 
 def as_sent(value):
@@ -106,7 +128,7 @@
         .astype(jnp.bfloat16)
         .reshape(4 * rows, quarter, D_ROPE)
     )
-    all_segs = lax.all_gather(segment_ids, "seq", axis=0, tiled=True)
+    all_segs = find_matrix_now(segment_ids)
     padded_segs = jnp.concatenate([jnp.full((REACH * rows,), -1, jnp.int32), all_segs], 0)
     first = place // 4 * 4
     window = (REACH + 1) * rows

time: 300 us -> 311 us (1.037)
  waiting for transfers between devices: 114 us -> 167 us
  blocking collectives: 83.7 us -> 32.4 us
  starting transfers between devices: 46.2 us -> 53.6 us
    ppermute x0 -> x7, waiting for transfers between devices: none -> 85.8 us  [extend_types_up(): val2 = lax.ppermute(passed[0], device_axis, ledger)]
    all_gather x1 -> x0, blocking collectives: 50.2 us -> none  [body(): all_segs = lax.all_gather(segment_ids, 'seq', axis=0, tiled=True)]
    all_to_all x1, waiting for transfers between devices: 34.9 us -> 0.01 us  [body(): lax.all_to_all(sent[1], 'seq', split_axis=0, concat_axis=1, tiled=True)]
    ppermute x0 -> x7, starting transfers between devices: none -> 13.1 us  [extend_types_up(): val2 = lax.ppermute(passed[0], device_axis, ledger)]
    ppermute x8, starting transfers between devices: 23.1 us -> 13.3 us  [from_partner(): return lax.ppermute(value, axis, pairs)]
    ppermute x2, starting transfers between devices: 6.85 us -> 10.8 us  [shifted(): return lax.ppermute(block, axis, route)]
  transfers between devices with their start and end apart: 13 -> 20, of which waited for: 6 -> 11; matrix products, arithmetic and copies ran while one was open for 10% -> 12% of each run, Pallas kernels for 0% -> 0%
where the time goes in v1:
time: 311 us
  waiting for transfers between devices  167 us (54%)
  starting transfers between devices  53.6 us (17%)
  blocking collectives  32.4 us (10%)
  matrix products  29.9 us (10%)
  local copies, waits for them, and re-layouts  16.2 us (5%)
  other arithmetic  9.44 us (3%)
    ppermute x7, waiting for transfers between devices, extend_types_up(): val2 = lax.ppermute(passed[0], device_axis, ledger)  85.8 us
    ppermute x8, waiting for transfers between devices, from_partner(): return lax.ppermute(value, axis, pairs)  56.6 us
    all_to_all x1, waiting for transfers between devices, body(): lax.all_to_all(sent[2], 'seq', split_axis=0, concat_axis=1, tiled=True)  25 us
    pmax x1, blocking collectives, body(): head_max = lax.pmax(local_heads, 'seq')  17.1 us
    ppermute x8, starting transfers between devices, from_partner(): return lax.ppermute(value, axis, pairs)  13.3 us
    ppermute x7, starting transfers between devices, extend_types_up(): val2 = lax.ppermute(passed[0], device_axis, ledger)  13.1 us
    dot_general x4, matrix products, score_max(): jnp.einsum('qhd,kd->hqk', query_rope, key_rope, preferred_element_type=jn...  11.2 us
    ppermute x2, starting transfers between devices, shifted(): return lax.ppermute(block, axis, route)  10.8 us
  transfers between devices with their start and end apart: 20, of which 11 were waited for; matrix products, arithmetic and copies ran while one was open for 12% of the time, Pallas kernels for 0%

profile of v1, /device:TPU:0, one launch (start us, length us, event | category | flops | bytes accessed | tf_op | source)
XLA Modules:
  0.0 310.7 jit_solution(7416090284505098747)
XLA Ops:
  0.6 1.5 reshape.406
  3.4 7.3 %all-to-all-start.1 = ((bf16[8,64,1024]{2,1,0:T(8,128)(2,1)}), bf16[8,64,1024]{2,1,0:T(8,128)(2,1)S(1)}, u32[]{:S(2)}, u32[]{:S(2)}) async-start(bf16[8,64,1024]{2,1,0:T(8,128)(2,1)} %bitcast.6), calls=%async_computation.1 | async-start | bytes 2097152 | tf_op jit(solution)/shard_map/all_to_all | solution.py:89
  11.5 25.0 %all-to-all-done.1 = bf16[8,64,1024]{2,1,0:T(8,128)(2,1)S(1)} async-done(((bf16[8,64,1024]{2,1,0:T(8,128)(2,1)}), bf16[8,64,1024]{2,1,0:T(8,128)(2,1)S(1)}, u32[]{:S(2)}, u32[]{:S(2)}) %all-to-all-start.1) | async-done | bytes 1048608 | tf_op jit(solution)/shard_map/all_to_all | solution.py:89
  36.5 1.4 tile.31
  37.9 4.4 %all-to-all-start.2 = ((bf16[8,192,512]{2,1,0:T(8,128)(2,1)}), bf16[8,192,512]{2,1,0:T(8,128)(2,1)}, u32[]{:S(2)}, u32[]{:S(2)}) async-start(bf16[8,192,512]{2,1,0:T(8,128)(2,1)} %bitcast.11), calls=%async_computation.2 | async-start | bytes 3145728 | tf_op jit(solution)/shard_map/all_to_all | solution.py:88
  42.3 1.9 collective-permute-start
  44.2 1.5 collective-permute-start.12
  45.7 6.3 %all_gather.7 = bf16[256,512]{1,0:T(8,128)(2,1)} all-gather(bf16[256,128]{1,0:T(8,128)(2,1)S(1)} %copy-done.15), channel_id=1, replica_groups=mesh['seq'=8,'head'=4] {'head'}, dimensions={1}, use_global_device_ids=true | all-gather | bytes 327680 | tf_op jit(solution)/shard_map/all_gather | solution.py:71
  52.5 9.0 %all_gather.6 = bf16[256,1536]{1,0:T(8,128)(2,1)} all-gather(bf16[256,384]{1,0:T(8,128)(2,1)S(1)} %copy-done.14), channel_id=1, replica_groups=mesh['seq'=8,'head'=4] {'head'}, dimensions={1}, use_global_device_ids=true | all-gather | bytes 983040 | tf_op jit(solution)/shard_map/all_gather | solution.py:70
  61.5 1.5 collective-permute-start.7
  63.1 9.2 %collective-permute-done = s32[256]{0:T(256)S(1)} collective-permute-done((s32[256]{0:T(256)S(1)}, s32[256]{0:T(256)S(1)}, u32[]{:S(2)}, u32[]{:S(2)}) %collective-permute-start) | collective-permute-done | bytes 1056 | tf_op jit(solution)/shard_map/ppermute | solution.py:24
  72.3 1.2 reshape.404
  74.0 9.5 %collective-permute-done.1 = s32[256]{0:T(256)S(1)} collective-permute-done((s32[256]{0:T(256)S(1)}, s32[256]{0:T(256)S(1)}, u32[]{:S(2)}, u32[]{:S(2)}) %collective-permute-start.1) | collective-permute-done | bytes 1056 | tf_op jit(solution)/shard_map/ppermute | solution.py:24
  83.5 2.5 collective-permute-start.2
  86.0 2.1 tile.12
  88.1 4.7 %all-to-all-start = ((bf16[8,192,1024]{2,1,0:T(8,128)(2,1)}), bf16[8,192,1024]{2,1,0:T(8,128)(2,1)}, u32[]{:S(2)}, u32[]{:S(2)}) async-start(bf16[8,192,1024]{2,1,0:T(8,128)(2,1)} %bitcast.2), calls=%async_computation | async-start | bytes 6291456 | tf_op jit(solution)/shard_map/all_to_all | solution.py:87
  92.9 2.1 collective-permute-start.3
  94.9 53.3 %collective-permute-done.3 = s32[256]{0:T(256)S(1)} collective-permute-done((s32[256]{0:T(256)S(1)}, s32[256]{0:T(256)S(1)}, u32[]{:S(2)}, u32[]{:S(2)}) %collective-permute-start.3) | collective-permute-done | bytes 1056 | tf_op jit(solution)/shard_map/ppermute | solution.py:24
  148.2 6.3 %collective-permute-done.4 = s32[256]{0:T(256)S(1)} collective-permute-done((s32[256]{0:T(256)S(1)}, s32[256]{0:T(256)S(1)}, u32[]{:S(2)}, u32[]{:S(2)}) %collective-permute-start.4) | collective-permute-done | bytes 1056 | tf_op jit(solution)/shard_map/ppermute | solution.py:24
  154.5 6.3 %collective-permute-done.5 = s32[256]{0:T(256)S(1)} collective-permute-done((s32[256]{0:T(256)S(1)}, s32[256]{0:T(256)S(1)}, u32[]{:S(2)}, u32[]{:S(2)}) %collective-permute-start.5) | collective-permute-done | bytes 1056 | tf_op jit(solution)/shard_map/ppermute | solution.py:24
  160.7 6.6 %collective-permute-start.6 = (s32[256]{0:T(256)S(1)}, s32[256]{0:T(256)S(1)}, u32[]{:S(2)}, u32[]{:S(2)}) collective-permute-start(s32[256]{0:T(256)S(1)} %collective-permute-done.5), channel_id=1, source_target_pairs={{0,4},{4,8},{8,12},{12,16},{16,20},{20,24},{24,28},{28,0},{1,5},{5... | collective-permute-start | bytes 3080 | tf_op jit(solution)/shard_map/ppermute | solution.py:24
  167.4 1.3 collective-permute-done.6
  168.9 1.3 maximum_select_fusion.5
  170.2 5.1 %collective-permute-start.10 = (bf16[512,512]{1,0:T(8,128)(2,1)S(1)}, bf16[512,512]{1,0:T(8,128)(2,1)S(1)}, u32[]{:S(2)}, u32[]{:S(2)}) collective-permute-start(bf16[512,512]{1,0:T(8,128)(2,1)S(1)} %maximum_select_fusion.5), channel_id=1, source_target_pairs={{0,8},{4,12},{8,0},{12,4},{16,24},{20,28},{24,16},{28,20},{1,9},{5... | collective-permute-start | bytes 1572872 | tf_op jit(solution)/shard_map/ppermute | solution.py:43
  176.1 8.1 %collective-permute-done.10 = bf16[512,512]{1,0:T(8,128)(2,1)S(1)} collective-permute-done((bf16[512,512]{1,0:T(8,128)(2,1)S(1)}, bf16[512,512]{1,0:T(8,128)(2,1)S(1)}, u32[]{:S(2)}, u32[]{:S(2)}) %collective-permute-start.10) | collective-permute-done | bytes 524320 | tf_op jit(solution)/shard_map/ppermute | solution.py:43
  184.7 7.6 %collective-permute-start.11 = (bf16[768,512]{1,0:T(8,128)(2,1)S(1)}, bf16[768,512]{1,0:T(8,128)(2,1)S(1)}, u32[]{:S(2)}, u32[]{:S(2)}) collective-permute-start(bf16[768,512]{1,0:T(8,128)(2,1)S(1)} %slice.117), channel_id=1, source_target_pairs={{0,16},{4,20},{8,24},{12,28},{1,17},{5,21},{9,25},{13,29},{2,18},{... | collective-permute-start | bytes 2359304 | tf_op jit(solution)/shard_map/ppermute | solution.py:49
  192.3 2.3 maximum_select_fusion.1
  195.3 1.8 collective-permute-start.13
  197.5 43.0 %collective-permute-done.13 = bf16[512,64]{0,1:T(8,128)(2,1)S(1)} collective-permute-done((bf16[512,64]{0,1:T(8,128)(2,1)S(1)}, bf16[512,64]{0,1:T(8,128)(2,1)S(1)}, u32[]{:S(2)}, u32[]{:S(2)}) %collective-permute-start.13) | collective-permute-done | bytes 65568 | tf_op jit(solution)/shard_map/ppermute | solution.py:43
  241.2 3.2 %collective-permute-start.14 = (bf16[768,64]{0,1:T(8,128)(2,1)}, bf16[768,64]{0,1:T(8,128)(2,1)}, u32[]{:S(2)}, u32[]{:S(2)}) collective-permute-start(bf16[768,64]{0,1:T(8,128)(2,1)} %slice.119), channel_id=1, source_target_pairs={{0,16},{4,20},{8,24},{12,28},{1,17},{5,21},{9,25},{13,29},{2,18},{... | collective-permute-start | bytes 294920 | tf_op jit(solution)/shard_map/ppermute | solution.py:49
  244.4 2.2 multiply_convert_fusion
  246.6 2.9 fusion.37
  249.6 3.9 %multiply_convert_fusion.3 = bf16[1024,512]{0,1:T(8,128)(2,1)S(1)} fusion(bf16[1536,512]{1,0:T(8,128)(2,1)} %bitcast.12, bf16[512,1536]{1,0:T(8,128)(2,1)S(1)} %maximum_select_fusion.1, bf16[512,1536]{1,0:T(8,128)(2,1)S(1)} %collective-permute-done.8, pred[]{:T(512)S(6)} %eq.85), kind=kOutput, calls=%fused_computation.20 | convolution fusion | flops 1625817088 | bytes 5767169 | tf_op jit(solution)/shard_map/dot_general | solution.py:127
  254.4 7.2 %multiply_convert_fusion.1 = bf16[1024,1024]{0,1:T(8,128)(2,1)S(1)} fusion(bf16[1536,1024]{1,0:T(8,128)(2,1)} %bitcast.3, bf16[512,1536]{1,0:T(8,128)(2,1)} %copy-done.8, bf16[512,1536]{1,0:T(8,128)(2,1)} %copy-done.19, pred[]{:T(512)S(6)} %eq.85), kind=kOutput, calls=%fused_computation.17 | convolution fusion | flops 3237478400 | bytes 8388609 | tf_op jit(solution)/shard_map/dot_general | solution.py:122
  261.8 1.4 copy-done.2
  263.2 1.3 fusion.44
  264.8 1.3 fusion.41
  266.4 1.3 fusion.43
  267.7 2.1 fusion.2
  269.9 1.5 fusion.42
  271.4 3.0 fusion.11
  274.5 2.9 fusion.5
  277.4 3.1 %fusion.8 = f32[8,256]{1,0:T(8,128)S(1)} fusion(f32[8,256,1024]{2,1,0:T(8,128)S(1)} %fusion.42, pred[256,1024]{1,0:T(8,128)(4,1)S(1)} %get-tuple-element.30, bf16[256,8,64]{0,2,1:T(8,128)(2,1)S(1)} %bitcast.105, bf16[1024,64]{0,1:T(8,128)(2,1)S(1)} %maximum_select_fusion.6, bf16[768,64]{0,1:T(8,128)(2,1)} %collective-permute-done.14), kind=kOutput, calls=%fused_computation.11 | convolution fusion | flops 277084160 | bytes 9150464 | tf_op jit(solution)/shard_map/qhd,kd->hqk/dot_general | solution.py:54
  280.6 3.9 %collective-permute-done.15 = f32[1,4,8,256]{3,2,0,1:T(8,128)S(1)} collective-permute-done((f32[1,4,8,256]{3,2,0,1:T(8,128)S(1)}, f32[1,4,8,256]{3,2,0,1:T(8,128)S(1)}, u32[]{:S(2)}, u32[]{:S(2)}) %collective-permute-start.15) | collective-permute-done | bytes 32800 | tf_op jit(solution)/shard_map/ppermute | solution.py:43
  284.5 2.5 collective-permute-start.16
  287.7 1.6 collective-permute-done.16
  290.0 17.1 %pmax.7 = f32[32]{0:T(128)S(1)} all-reduce(f32[32]{0:T(128)S(1)} %reduce_max.52), channel_id=1, replica_groups=mesh['seq'=8,'head'=4] {'seq'}, use_global_device_ids=true, to_apply=%region_5.6 | all-reduce | flops 32 | bytes 256 | tf_op jit(solution)/shard_map/pmax | solution.py:165
  308.1 1.5 multiply_convert_fusion.2
  (111 shorter events, 10.9 us)
Async XLA Ops:
  0.6 10.1 %copy-start.5 = (bf16[192,2048]{1,0:T(8,128)(2,1)S(1)}, bf16[192,2048]{1,0:T(8,128)(2,1)}, u32[]{:S(2)}) copy-start(bf16[192,2048]{1,0:T(8,128)(2,1)} %param.13) | copy-start | bytes 2359300
  3.4 33.0 %all-to-all-start.1 = ((bf16[8,64,1024]{2,1,0:T(8,128)(2,1)}), bf16[8,64,1024]{2,1,0:T(8,128)(2,1)S(1)}, u32[]{:S(2)}, u32[]{:S(2)}) async-start(bf16[8,64,1024]{2,1,0:T(8,128)(2,1)} %bitcast.6), calls=%async_computation.1 | async-start | bytes 2097152 | tf_op jit(solution)/shard_map/all_to_all | solution.py:89
  11.4 30.9 %copy-start.17 = (s32[256]{0:T(256)S(1)}, s32[256]{0:T(256)}, u32[]{:S(2)}) copy-start(s32[256]{0:T(256)} %param.11) | copy-start | bytes 3076
  11.4 32.8 %copy-start.16 = (bf16[256,64]{0,1:T(8,128)(2,1)S(1)}, bf16[256,64]{0,1:T(8,128)(2,1)}, u32[]{:S(2)}) copy-start(bf16[256,64]{0,1:T(8,128)(2,1)} %param.10) | copy-start | bytes 98308
  11.5 34.2 %copy-start.15 = (bf16[256,128]{1,0:T(8,128)(2,1)S(1)}, bf16[256,128]{1,0:T(8,128)(2,1)}, u32[]{:S(2)}) copy-start(bf16[256,128]{1,0:T(8,128)(2,1)} %param.9) | copy-start | bytes 196612
  11.5 60.8 %copy-start.3 = (bf16[192,4096]{1,0:T(8,128)(2,1)S(1)}, bf16[192,4096]{1,0:T(8,128)(2,1)}, u32[]{:S(2)}) copy-start(bf16[192,4096]{1,0:T(8,128)(2,1)} %param.12) | copy-start | bytes 4718596
  36.5 25.1 %copy-start.9 = (bf16[8,64,1024]{2,1,0:T(8,128)(2,1)}, bf16[8,64,1024]{2,1,0:T(8,128)(2,1)S(1)}, u32[]{:S(2)}) copy-start(bf16[8,64,1024]{2,1,0:T(8,128)(2,1)S(1)} %all-to-all-done.1) | copy-start | bytes 3145732
  37.9 14.6 %copy-start.14 = (bf16[256,384]{1,0:T(8,128)(2,1)S(1)}, bf16[256,384]{1,0:T(8,128)(2,1)}, u32[]{:S(2)}) copy-start(bf16[256,384]{1,0:T(8,128)(2,1)} %param.8) | copy-start | bytes 589828
  37.9 48.1 %all-to-all-start.2 = ((bf16[8,192,512]{2,1,0:T(8,128)(2,1)}), bf16[8,192,512]{2,1,0:T(8,128)(2,1)}, u32[]{:S(2)}, u32[]{:S(2)}) async-start(bf16[8,192,512]{2,1,0:T(8,128)(2,1)} %bitcast.11), calls=%async_computation.2 | async-start | bytes 3145728 | tf_op jit(solution)/shard_map/all_to_all | solution.py:88
  42.3 30.0 %collective-permute-start = (s32[256]{0:T(256)S(1)}, s32[256]{0:T(256)S(1)}, u32[]{:S(2)}, u32[]{:S(2)}) collective-permute-start(s32[256]{0:T(256)S(1)} %copy-done.17), channel_id=1, source_target_pairs={{0,4},{4,8},{8,12},{12,16},{16,20},{20,24},{24,28},{28,0},{1,5},{5... | collective-permute-start | bytes 3080 | tf_op jit(solution)/shard_map/ppermute | solution.py:24
  44.2 151.1 %collective-permute-start.12 = (bf16[256,64]{0,1:T(8,128)(2,1)S(1)}, bf16[256,64]{0,1:T(8,128)(2,1)S(1)}, u32[]{:S(2)}, u32[]{:S(2)}) collective-permute-start(bf16[256,64]{0,1:T(8,128)(2,1)S(1)} %copy-done.16), channel_id=1, source_target_pairs={{0,4},{4,0},{8,12},{12,8},{16,20},{20,16},{24,28},{28,24},{1,5},{5... | collective-permute-start | bytes 98312 | tf_op jit(solution)/shard_map/ppermute | solution.py:43
  51.9 116.9 %collective-permute-start.9 = (bf16[256,512]{1,0:T(8,128)(2,1)}, bf16[256,512]{1,0:T(8,128)(2,1)}, u32[]{:S(2)}, u32[]{:S(2)}) collective-permute-start(bf16[256,512]{1,0:T(8,128)(2,1)} %all_gather.7), channel_id=1, source_target_pairs={{0,4},{4,0},{8,12},{12,8},{16,20},{20,16},{24,28},{28,24},{1,5},{5... | collective-permute-start | bytes 786440 | tf_op jit(solution)/shard_map/ppermute | solution.py:43
  61.5 130.8 %collective-permute-start.7 = (bf16[256,1536]{1,0:T(8,128)(2,1)}, bf16[256,1536]{1,0:T(8,128)(2,1)}, u32[]{:S(2)}, u32[]{:S(2)}) collective-permute-start(bf16[256,1536]{1,0:T(8,128)(2,1)} %all_gather.6), channel_id=1, source_target_pairs={{0,4},{4,0},{8,12},{12,8},{16,20},{20,16},{24,28},{28,24},{1,5},{5... | collective-permute-start | bytes 2359304 | tf_op jit(solution)/shard_map/ppermute | solution.py:43
  72.3 11.2 %collective-permute-start.1 = (s32[256]{0:T(256)S(1)}, s32[256]{0:T(256)S(1)}, u32[]{:S(2)}, u32[]{:S(2)}) collective-permute-start(s32[256]{0:T(256)S(1)} %collective-permute-done), channel_id=1, source_target_pairs={{0,4},{4,8},{8,12},{12,16},{16,20},{20,24},{24,28},{28,0},{1,5},{5... | collective-permute-start | bytes 3080 | tf_op jit(solution)/shard_map/ppermute | solution.py:24
  83.5 9.4 %collective-permute-start.2 = (s32[256]{0:T(256)S(1)}, s32[256]{0:T(256)S(1)}, u32[]{:S(2)}, u32[]{:S(2)}) collective-permute-start(s32[256]{0:T(256)S(1)} %collective-permute-done.1), channel_id=1, source_target_pairs={{0,4},{4,8},{8,12},{12,16},{16,20},{20,24},{24,28},{28,0},{1,5},{5... | collective-permute-start | bytes 3080 | tf_op jit(solution)/shard_map/ppermute | solution.py:24
  88.1 166.3 %all-to-all-start = ((bf16[8,192,1024]{2,1,0:T(8,128)(2,1)}), bf16[8,192,1024]{2,1,0:T(8,128)(2,1)}, u32[]{:S(2)}, u32[]{:S(2)}) async-start(bf16[8,192,1024]{2,1,0:T(8,128)(2,1)} %bitcast.2), calls=%async_computation | async-start | bytes 6291456 | tf_op jit(solution)/shard_map/all_to_all | solution.py:87
  92.9 55.3 %collective-permute-start.3 = (s32[256]{0:T(256)S(1)}, s32[256]{0:T(256)S(1)}, u32[]{:S(2)}, u32[]{:S(2)}) collective-permute-start(s32[256]{0:T(256)S(1)} %collective-permute-done.2), channel_id=1, source_target_pairs={{0,4},{4,8},{8,12},{12,16},{16,20},{20,24},{24,28},{28,0},{1,5},{5... | collective-permute-start | bytes 3080 | tf_op jit(solution)/shard_map/ppermute | solution.py:24
  148.2 6.3 %collective-permute-start.4 = (s32[256]{0:T(256)S(1)}, s32[256]{0:T(256)S(1)}, u32[]{:S(2)}, u32[]{:S(2)}) collective-permute-start(s32[256]{0:T(256)S(1)} %collective-permute-done.3), channel_id=1, source_target_pairs={{0,4},{4,8},{8,12},{12,16},{16,20},{20,24},{24,28},{28,0},{1,5},{5... | collective-permute-start | bytes 3080 | tf_op jit(solution)/shard_map/ppermute | solution.py:24
  154.5 6.3 %collective-permute-start.5 = (s32[256]{0:T(256)S(1)}, s32[256]{0:T(256)S(1)}, u32[]{:S(2)}, u32[]{:S(2)}) collective-permute-start(s32[256]{0:T(256)S(1)} %collective-permute-done.4), channel_id=1, source_target_pairs={{0,4},{4,8},{8,12},{12,16},{16,20},{20,24},{24,28},{28,0},{1,5},{5... | collective-permute-start | bytes 3080 | tf_op jit(solution)/shard_map/ppermute | solution.py:24
  160.7 7.9 %collective-permute-start.6 = (s32[256]{0:T(256)S(1)}, s32[256]{0:T(256)S(1)}, u32[]{:S(2)}, u32[]{:S(2)}) collective-permute-start(s32[256]{0:T(256)S(1)} %collective-permute-done.5), channel_id=1, source_target_pairs={{0,4},{4,8},{8,12},{12,16},{16,20},{20,24},{24,28},{28,0},{1,5},{5... | collective-permute-start | bytes 3080 | tf_op jit(solution)/shard_map/ppermute | solution.py:24
  170.2 14.0 %collective-permute-start.10 = (bf16[512,512]{1,0:T(8,128)(2,1)S(1)}, bf16[512,512]{1,0:T(8,128)(2,1)S(1)}, u32[]{:S(2)}, u32[]{:S(2)}) collective-permute-start(bf16[512,512]{1,0:T(8,128)(2,1)S(1)} %maximum_select_fusion.5), channel_id=1, source_target_pairs={{0,8},{4,12},{8,0},{12,4},{16,24},{20,28},{24,16},{28,20},{1,9},{5... | collective-permute-start | bytes 1572872 | tf_op jit(solution)/shard_map/ppermute | solution.py:43
  184.7 59.7 %copy-start.10 = (bf16[8,64,1024]{2,1,0:T(8,128)(2,1)S(1)}, bf16[8,64,1024]{2,1,0:T(8,128)(2,1)}, u32[]{:S(2)}) copy-start(bf16[8,64,1024]{2,1,0:T(8,128)(2,1)} %copy-done.9) | copy-start | bytes 3145732
  184.7 59.7 %collective-permute-start.11 = (bf16[768,512]{1,0:T(8,128)(2,1)S(1)}, bf16[768,512]{1,0:T(8,128)(2,1)S(1)}, u32[]{:S(2)}, u32[]{:S(2)}) collective-permute-start(bf16[768,512]{1,0:T(8,128)(2,1)S(1)} %slice.117), channel_id=1, source_target_pairs={{0,16},{4,20},{8,24},{12,28},{1,17},{5,21},{9,25},{13,29},{2,18},{... | collective-permute-start | bytes 2359304 | tf_op jit(solution)/shard_map/ppermute | solution.py:49
  194.6 54.9 %copy-start.8 = (bf16[512,1536]{1,0:T(8,128)(2,1)}, bf16[512,1536]{1,0:T(8,128)(2,1)S(1)}, u32[]{:S(2)}) copy-start(bf16[512,1536]{1,0:T(8,128)(2,1)S(1)} %maximum_select_fusion.1) | copy-start | bytes 4718596
  194.6 54.9 %collective-permute-start.8 = (bf16[512,1536]{1,0:T(8,128)(2,1)S(1)}, bf16[512,1536]{1,0:T(8,128)(2,1)S(1)}, u32[]{:S(2)}, u32[]{:S(2)}) collective-permute-start(bf16[512,1536]{1,0:T(8,128)(2,1)S(1)} %maximum_select_fusion.1), channel_id=1, source_target_pairs={{0,8},{4,12},{8,0},{12,4},{16,24},{20,28},{24,16},{28,20},{1,9},{5... | collective-permute-start | bytes 4718600 | tf_op jit(solution)/shard_map/ppermute | solution.py:43
  195.3 45.2 %collective-permute-start.13 = (bf16[512,64]{0,1:T(8,128)(2,1)S(1)}, bf16[512,64]{0,1:T(8,128)(2,1)S(1)}, u32[]{:S(2)}, u32[]{:S(2)}) collective-permute-start(bf16[512,64]{0,1:T(8,128)(2,1)S(1)} %maximum_select_fusion.7), channel_id=1, source_target_pairs={{0,8},{4,12},{8,0},{12,4},{16,24},{20,28},{24,16},{28,20},{1,9},{5... | collective-permute-start | bytes 196616 | tf_op jit(solution)/shard_map/ppermute | solution.py:43
  241.2 30.2 %collective-permute-start.14 = (bf16[768,64]{0,1:T(8,128)(2,1)}, bf16[768,64]{0,1:T(8,128)(2,1)}, u32[]{:S(2)}, u32[]{:S(2)}) collective-permute-start(bf16[768,64]{0,1:T(8,128)(2,1)} %slice.119), channel_id=1, source_target_pairs={{0,16},{4,20},{8,24},{12,28},{1,17},{5,21},{9,25},{13,29},{2,18},{... | collective-permute-start | bytes 294920 | tf_op jit(solution)/shard_map/ppermute | solution.py:49
  249.5 3.9 %copy-start.19 = (bf16[512,1536]{1,0:T(8,128)(2,1)}, bf16[512,1536]{1,0:T(8,128)(2,1)S(1)}, u32[]{:S(2)}) copy-start(bf16[512,1536]{1,0:T(8,128)(2,1)S(1)} %collective-permute-done.8) | copy-start | bytes 4718596
  261.7 1.6 copy-start.2
  263.2 1.6 copy-start.1
  264.8 1.6 copy-start
  266.4 1.3 copy-start.13
  269.9 1.5 copy-start.12
  271.4 3.1 copy-start.11
  277.3 29.9 %copy-start.7 = (bf16[64,4096]{1,0:T(8,128)(2,1)S(1)}, bf16[64,4096]{1,0:T(8,128)(2,1)}, u32[]{:S(2)}) copy-start(bf16[64,4096]{1,0:T(8,128)(2,1)} %param.14) | copy-start | bytes 1572868
  277.4 30.7 %copy-start.4 = (bf16[192,4096]{1,0:T(8,128)(2,1)S(1)}, bf16[192,4096]{1,0:T(8,128)(2,1)}, u32[]{:S(2)}) copy-start(bf16[192,4096]{1,0:T(8,128)(2,1)} %param.12) | copy-start | bytes 4718596
  280.5 29.2 %copy-start.6 = (bf16[192,2048]{1,0:T(8,128)(2,1)S(1)}, bf16[192,2048]{1,0:T(8,128)(2,1)}, u32[]{:S(2)}) copy-start(bf16[192,2048]{1,0:T(8,128)(2,1)} %param.13) | copy-start | bytes 2359300
  280.5 4.0 %collective-permute-start.15 = (f32[1,4,8,256]{3,2,0,1:T(8,128)S(1)}, f32[1,4,8,256]{3,2,0,1:T(8,128)S(1)}, u32[]{:S(2)}, u32[]{:S(2)}) collective-permute-start(f32[1,4,8,256]{3,2,0,1:T(8,128)S(1)} %maximum_bitcast_fusion), channel_id=1, source_target_pairs={{0,4},{4,0},{8,12},{12,8},{16,20},{20,16},{24,28},{28,24},{1,5},{5... | collective-permute-start | bytes 98312 | tf_op jit(solution)/shard_map/ppermute | solution.py:43
  284.5 4.8 %collective-permute-start.16 = (f32[2,4,8,256]{3,2,0,1:T(8,128)S(1)}, f32[2,4,8,256]{3,2,0,1:T(8,128)S(1)}, u32[]{:S(2)}, u32[]{:S(2)}) collective-permute-start(f32[2,4,8,256]{3,2,0,1:T(8,128)S(1)} %maximum_select_fusion.8), channel_id=1, source_target_pairs={{0,8},{4,12},{8,0},{12,4},{16,24},{20,28},{24,16},{28,20},{1,9},{5... | collective-permute-start | bytes 196616 | tf_op jit(solution)/shard_map/ppermute | solution.py:43
  307.1 3.6 %copy-start.18 = (f32[32]{0:T(128)}, f32[32]{0:T(128)S(1)}, u32[]{:S(2)}) copy-start(f32[32]{0:T(128)S(1)} %pmax.7) | copy-start | bytes 388
